TPU v7x, 32 devices: a whole 2x2x4 slice. The times are simulated.
32 devices in a mesh: cfg: 2 (over y), space: 4 (over z), tm: 4 (over x, core).
Axes of the slice: x: 2, y: 2, z: 4, core: 2. Of those that a mesh axis runs over, the one named last changes fastest.
Arguments:
- solutions: bfloat16 [16, 128, 32, 3072], P(('cfg', 'tm'), None, None, 'space'), parts along dimension 0, may hold values from -6 to 6
- eigvecs: bfloat16 [16, 2, 128, 3072], P(('cfg', 'tm'), None, 'space'), parts along dimension 0, may hold values from -0.078125 to 0.078125
- source_time: int32 [256], P('cfg'), parts along dimension 0, may hold values from 0 to 7
Outputs:
- perambulator: bfloat16 [16, 128, 32, 128], P(('cfg', 'tm'), 'space'), parts along dimension 0
There are 2 independent parts, one for each index of `cfg`. A program takes and returns all parts, laid end to end along the dimension named above; each array names one. Nothing has to cross between parts.
All inputs are finite; a program needn't handle non-finite values.
Results may differ from a plain program's by a relative error of at most 0.001.
Values may be sent and summed in bfloat16 or wider, within the bound.
A program may use at most 128 MiB of HBM per device.

v0:
```python
import functools

import jax
import jax.numpy as jnp
from jax import lax
from jax.experimental import pallas as pl
from jax.experimental.pallas import tpu as pltpu
from jax.sharding import PartitionSpec as P

MESH = pl.DeviceIdType.MESH
LEVELS = 32767.0
PIECES = 1
STEP = 0.6931471805599453 / 16


def kernel(n, pieces, time_hbm, sol_ref, eig_hbm, out_ref, time_ref, eig_ref, sol_v, eig_v, w_v, part, own, code,
           code_in, time_sem, load_sem, sol_sem, own_sem, eig_send, eig_recv, code_send, code_recv):
    me = lax.axis_index("space")
    slices, sources, spins, cols = sol_v.shape
    count = eig_ref.shape[2]
    vectors = n * count
    owned = sources // n
    piece = owned // pieces
    rows = piece * spins
    half = spins // 2
    outer = jnp.where(me < n // 2, me - 1, me + 1)
    is_end = (me == 0) | (me == n - 1)

    barrier = pltpu.get_barrier_semaphore()
    for o in range(1, n):
        pl.semaphore_signal(barrier, inc=1, device_id={"space": lax.rem(me + o, n)}, device_id_type=MESH)

    def block_of(d):
        return pl.ds(pl.multiple_of(d * cols, cols), cols)

    def eig_own(t):
        return pltpu.make_async_copy(eig_hbm.at[t, :, :, block_of(me)], eig_v.at[t, me], own_sem.at[t])

    def eig_load(t):
        return pltpu.make_async_copy(eig_hbm.at[t], eig_ref.at[t], load_sem.at[t])

    def sol_copy(t, d):
        rows = pl.ds(d * owned, owned)
        return pltpu.make_async_copy(sol_ref.at[t, rows], sol_v.at[t, rows], sol_sem.at[t, d])

    def eig_copy(t, o, dst):
        to = lax.rem(me + o, n)
        return pltpu.make_async_remote_copy(
            eig_ref.at[t, :, :, block_of(to)], eig_v.at[t, dst], eig_send.at[t, o], eig_recv.at[t, o],
            device_id={"space": to}, device_id_type=MESH)

    for t in range(slices):
        eig_load(t).start()
    time_copy = pltpu.make_async_copy(time_hbm, time_ref, time_sem)
    time_copy.start()
    for t in range(slices):
        eig_own(t).start()

    def start_sol(t):
        def body(d, _):
            sol_copy(t, d).start()
            return 0
        lax.fori_loop(0, n, body, 0)

    far_first = sorted(range(1, n), key=lambda o: -min(o, n - o))
    eig_load(0).wait()
    pl.semaphore_wait(barrier, n - 1)
    for o in far_first:
        eig_copy(0, o, me).start()
    for t in range(slices):
        start_sol(t)
    for t in range(1, slices):
        eig_load(t).wait()
    time_copy.wait()

    def partial_sum(t, q, dst):
        block = sol_v[t, pl.ds(q * piece, piece)].reshape(piece * spins, cols)
        p = lax.dot_general(block, w_v[t], (((1,), (1,)), ((), ())), preferred_element_type=jnp.float32)
        p = p.reshape(piece, 2, half, 2 * vectors)
        dst[:, :half, :] = p[:, 0, :, :vectors] + p[:, 1, :, vectors:]
        dst[:, half:, :] = p[:, 1, :, :vectors] - p[:, 0, :, vectors:]

    def chunk_copy(way, t, q):
        to = lax.rem(jnp.where(way == 0, me + 1, me + n - 1), n)
        return pltpu.make_async_remote_copy(
            code.at[t, q], code_in.at[way, t, q], code_send.at[t, q], code_recv.at[way, t, q],
            device_id={"space": to}, device_id_type=MESH)

    def received(way, t, q):
        chunk_copy(way, t, q).wait_recv()
        steps = code_in[way, t, q, rows:].astype(jnp.int32).astype(jnp.float32)[:1]
        value = code_in[way, t, q, :rows].astype(jnp.int32).astype(jnp.float32) * (jnp.exp(steps * STEP) * (1.0 / LEVELS))
        return value.reshape(piece, spins, vectors)

    def emit(t, way, d, i):
        q = d * pieces + i
        partial_sum(t, q, part)

        @pl.when(jnp.where(way == 0, me, n - 1 - me) > 0)
        def _():
            part[...] += received(way, t, q)

        x = part[...].reshape(rows, vectors)
        top = jnp.maximum(jnp.max(jnp.abs(x), axis=0, keepdims=True), 1e-30)
        steps = jnp.floor(jnp.log(top) * (1.0 / STEP)) + 2.0
        code[t, q, :rows] = jnp.round(x * (LEVELS * jnp.exp(steps * -STEP))).astype(jnp.int32).astype(jnp.int16)
        code[t, q, rows:] = jnp.broadcast_to(steps, (16, vectors)).astype(jnp.int32).astype(jnp.int16)
        chunk_copy(way, t, q).start()

    def emit_first(t):
        def body(j, _):
            k = j // (2 * pieces)
            way = jnp.where(me < n // 2, j % 2, 1 - j % 2)
            d = jnp.where(way == 0, n - 1 - k, k)
            least = jnp.where(is_end, 1, 0)

            @pl.when(jnp.where(way == 0, d - me, me - d) > least)
            def _():
                emit(t, way, d, (j // 2) % pieces)
            return 0

        lax.fori_loop(0, 2 * pieces * (n - 1), body, 0)

    def emit_last():
        def body(j, _):
            way = jnp.where(me == 0, 0, 1)
            emit(j // pieces, way, jnp.where(me == 0, 1, n - 2), j % pieces)
            return 0

        @pl.when(is_end)
        def _():
            lax.fori_loop(0, slices * pieces, body, 0)

    def forward(t):
        for o in range(1, n):
            eig_copy(t - 1, o, me).wait_send()
        for o in far_first[::-1]:
            eig_copy(t, o, me).start()

    for t in range(slices):
        if t + 1 < slices:
            @pl.when(is_end)
            def _():
                forward(t + 1)
        else:
            for o in range(1, n):
                eig_copy(t, o, me).wait_send()
        for o in range(1, n):
            source = lax.rem(me + n - o, n)
            if t == 0:
                eig_copy(t, o, source).wait_recv()
            else:
                @pl.when(is_end | (source != outer))
                def _():
                    eig_copy(t, o, source).wait_recv()
        if t + 1 < slices:
            @pl.when(jnp.logical_not(is_end))
            def _():
                o = lax.rem(me + n - outer, n)
                eig_copy(t + 1, o, outer).wait_recv()
                forward(t + 1)
        eig_own(t).wait()
        for c in range(2):
            w_v[t, c * vectors:(c + 1) * vectors, :] = (
                eig_v[t, :, c].astype(jnp.float32).reshape(vectors, cols).astype(jnp.bfloat16))

        def wait_sol(d, _):
            sol_copy(t, d).wait()
            return 0

        lax.fori_loop(0, n, wait_sol, 0)
        emit_first(t)
        if t + 1 == slices:
            emit_last()

        def own_sum(i, _):
            partial_sum(t, me * pieces + i, own.at[t, i])
            return 0

        lax.fori_loop(0, pieces, own_sum, 0)

    def finish(j, _):
        t, i = j // pieces, j % pieces

        @pl.when(me > 0)
        def _():
            own[t, i] += received(0, t, me * pieces + i)

        @pl.when(me < n - 1)
        def _():
            own[t, i] += received(1, t, me * pieces + i)

        now = lax.axis_index("tm") * slices + t
        for b in range(piece):
            sign = jnp.where(now < time_ref[me * owned + i * piece + b], -1.0, 1.0)
            out_ref[t, i * piece + b] = (own[t, i, b] * sign).astype(jnp.bfloat16)
        return 0

    lax.fori_loop(0, slices * pieces, finish, 0)

    def drain(j, _):
        t, q = j // (n * pieces), j % (n * pieces)
        d = q // pieces

        @pl.when(d != me)
        def _():
            chunk_copy(jnp.where(d > me, 0, 1), t, q).wait_send()
        return 0

    lax.fori_loop(0, slices * n * pieces, drain, 0)


def shards(n, solutions, eigvecs, source_time):
    slices, sources, spins, cols = solutions.shape
    count = eigvecs.shape[2]
    vectors = n * count
    owned = sources // n
    pieces = PIECES if owned % PIECES == 0 else 1
    piece = owned // pieces
    blocks = n * pieces
    dma = pltpu.SemaphoreType.DMA
    return pl.pallas_call(
        functools.partial(kernel, n, pieces),
        out_shape=jax.ShapeDtypeStruct((slices, owned, spins, vectors), jnp.bfloat16),
        in_specs=[
            pl.BlockSpec(memory_space=pltpu.HBM),
            pl.BlockSpec(memory_space=pltpu.HBM),
            pl.BlockSpec(memory_space=pltpu.HBM),
        ],
        out_specs=pl.BlockSpec(memory_space=pltpu.VMEM),
        scratch_shapes=[
            pltpu.SMEM(source_time.shape, jnp.int32),
            pltpu.VMEM(eigvecs.shape, jnp.bfloat16),
            pltpu.VMEM((slices, sources, spins, cols), jnp.bfloat16),
            pltpu.VMEM((slices, n, 2, count, cols), jnp.bfloat16),
            pltpu.VMEM((slices, 2 * vectors, cols), jnp.bfloat16),
            pltpu.VMEM((piece, spins, vectors), jnp.float32),
            pltpu.VMEM((slices, pieces, piece, spins, vectors), jnp.float32),
            pltpu.VMEM((slices, blocks, piece * spins + 16, vectors), jnp.int16),
            pltpu.VMEM((2, slices, blocks, piece * spins + 16, vectors), jnp.int16),
            dma,
            dma((slices,)),
            dma((slices, n)),
            dma((slices,)),
            dma((slices, n)),
            dma((slices, n)),
            dma((slices, blocks)),
            dma((2, slices, blocks)),
        ],
        compiler_params=pltpu.CompilerParams(
            collective_id=0, has_side_effects=True, vmem_limit_bytes=48 << 20),
    )(source_time, solutions, eigvecs)


def solution(mesh):
    return jax.shard_map(
        functools.partial(shards, mesh.shape["space"]),
        mesh=mesh,
        in_specs=(
            P(("cfg", "tm"), None, None, "space"),
            P(("cfg", "tm"), None, "space", None),
            P("cfg"),
        ),
        out_specs=P(("cfg", "tm"), "space", None, None),
        check_vma=False,
    )
```

profile of v0, /device:TPU:0, one launch (start us, length us, event | category | flops | bytes accessed | tf_op | source)
XLA Modules:
  0.0 55.1 jit_solution(8181049098283432933)
XLA Ops:
  0.0 0.0 copy-start
  0.0 1.1 %copy-done = bf16[2,2,32,3072]{3,2,1,0:T(8,128)(2,1)S(1)} copy-done((bf16[2,2,32,3072]{3,2,1,0:T(8,128)(2,1)S(1)}, bf16[2,2,32,3072]{3,2,1,0:T(8,128)(2,1)}, u32[]{:S(2)}) %copy-start) | copy-done | bytes 786456
  1.1 0.0 copy-start.1
  1.1 0.7 %copy-done.1 = s32[128]{0:T(128)S(1)} copy-done((s32[128]{0:T(128)S(1)}, s32[128]{0:T(128)}, u32[]{:S(2)}) %copy-start.1) | copy-done | bytes 536
  1.8 52.5 %shard_map.37 = bf16[2,32,32,128]{3,2,1,0:T(8,128)(2,1)S(1)} custom-call(s32[128]{0:T(128)S(1)} %copy-done.1, bf16[2,128,32,768]{3,2,1,0:T(8,128)(2,1)} %sol_ref.1, bf16[2,2,32,3072]{3,2,1,0:T(8,128)(2,1)S(1)} %copy-done), custom_call_target="tpu_custom_call" | custom-call | tf_op jit(solution)/shard_map/pallas_call | solution.py:222
  54.3 0.8 %copy.5 = bf16[2,32,32,128]{3,2,1,0:T(8,128)(2,1)} copy(bf16[2,32,32,128]{3,2,1,0:T(8,128)(2,1)S(1)} %shard_map.37) | data formatting | bytes 1048576
Async XLA Ops:
  0.0 1.1 %copy-start = (bf16[2,2,32,3072]{3,2,1,0:T(8,128)(2,1)S(1)}, bf16[2,2,32,3072]{3,2,1,0:T(8,128)(2,1)}, u32[]{:S(2)}) copy-start(bf16[2,2,32,3072]{3,2,1,0:T(8,128)(2,1)} %eig_hbm.1) | copy-start | bytes 2359300
  1.1 0.7 %copy-start.1 = (s32[128]{0:T(128)S(1)}, s32[128]{0:T(128)}, u32[]{:S(2)}) copy-start(s32[128]{0:T(128)} %time_hbm.1) | copy-start | bytes 1540
where the time goes:
time: 55.2 us; the launch traced here: 55.1 us
  Pallas kernels  52.5 us (95%)
  local copies, waits for them, and re-layouts  2.58 us (5%)
    pallas_call x1, Pallas kernels, shards(): pl.pallas_call(functools.partial(kernel, n, pieces), out_shape=jax.ShapeD...  52.5 us
    unnamed x5, local copies, waits for them, and re-layouts  2.58 us

commit v1 on v0

v1 whole, which is shorter than its diff:
```python
import functools

import jax
import jax.numpy as jnp
from jax import lax
from jax.experimental import pallas as pl
from jax.experimental.pallas import tpu as pltpu
from jax.sharding import PartitionSpec as P

MESH = pl.DeviceIdType.MESH
LEVELS = 32767.0
PIECES = 1
VMEM_BYTES = 67043328


def kernel(n, pieces, time_hbm, sol_hbm, eig_hbm, out_ref, time_ref, eig_v, sol_v, part, own, code, code_in, head,
           head_in, time_sem, load_sem, sol_sem, eig_send, eig_recv, code_send, code_recv, head_send, head_recv):
    me = lax.axis_index("space")
    slices, sources, spins, cols = sol_v.shape
    count = eig_v.shape[4]
    vectors = n * count
    owned = sources // n
    piece = owned // pieces
    rows = piece * spins
    half = spins // 2
    blocks = slices * pieces
    mirror = n - 1 - me

    barrier = pltpu.get_barrier_semaphore()

    def next_of(way):
        return me + 1 if way == 0 else me - 1

    def behind(way):
        return me if way == 0 else mirror

    for way in range(2):
        @pl.when(behind(1 - way) > 0)
        def _():
            pl.semaphore_signal(barrier, inc=1, device_id={"space": next_of(way)}, device_id_type=MESH)

    def eig_load(t, d):
        block = pl.ds(pl.multiple_of(d * cols, cols), cols)
        return pltpu.make_async_copy(eig_hbm.at[t, :, :, block], eig_v.at[t, d, :, me], load_sem.at[t, d])

    def sol_copy(t, d):
        owner = pl.ds(d * owned, owned)
        return pltpu.make_async_copy(sol_hbm.at[t, owner], sol_v.at[t, owner], sol_sem.at[t, d])

    def eig_copy(way, t, d, c, s):
        return pltpu.make_async_remote_copy(
            eig_v.at[t, d, c, s], eig_v.at[t, d, c, s], eig_send.at[t, d, c, s], eig_recv.at[t, d, c, s],
            device_id={"space": next_of(way)}, device_id_type=MESH)

    def each(total, body):
        def step(i, _):
            body(i)
            return 0
        lax.fori_loop(0, total, step, 0)

    each(slices * n, lambda i: eig_load(i % slices, i // slices).start())
    time_copy = pltpu.make_async_copy(time_hbm, time_ref, time_sem)
    time_copy.start()
    each(slices * n, lambda i: eig_load(i % slices, i // slices).wait())
    pl.semaphore_wait(barrier, jnp.where((me > 0) & (mirror > 0), 2, 1))

    def message(way, i):
        members = behind(way) + 1
        slot = i // members
        t, far, back = slot % slices, slot // slices, i % members
        if way == 0:
            return t, n - 1 - far, me - back, far < mirror
        return t, far, me + back, far < me

    def send_eigs(i):
        for c in range(2):
            for way in range(2):
                t, d, s, valid = message(way, i)

                @pl.when(valid)
                def _():
                    @pl.when(s != me)
                    def _():
                        eig_copy(way, t, d, c, s).wait_recv()

                    eig_copy(way, t, d, c, s).start()

    send_eigs(0)
    each(slices * n, lambda i: sol_copy(i // n, i % n).start())
    messages = slices * ((n * n) // 4)
    each(messages - 1, lambda i: send_eigs(i + 1))

    def wait_eigs(t):
        def body(i):
            s = i // 2

            @pl.when(s != me)
            def _():
                eig_copy(0, t, me, i % 2, s).wait_recv()

        each(2 * n, body)

    wait_eigs(0)
    each(slices * n, lambda i: sol_copy(i // n, i % n).wait())
    time_copy.wait()

    def partial_sum(t, q, dst):
        block = sol_v[t, pl.ds(q * piece, piece)].reshape(rows, cols)
        w = eig_v[t, me]
        if count % 16:
            w = w.astype(jnp.float32)
        w = w.reshape(2 * vectors, cols).astype(jnp.bfloat16)
        p = lax.dot_general(block, w, (((1,), (1,)), ((), ())), preferred_element_type=jnp.float32)
        p = p.reshape(piece, 2, half, 2 * vectors)
        dst[:, :half, :] = p[:, 0, :, :vectors] + p[:, 1, :, vectors:]
        dst[:, half:, :] = p[:, 1, :, :vectors] - p[:, 0, :, vectors:]

    def chunk_copy(way, t, q):
        return pltpu.make_async_remote_copy(
            code.at[t, q], code_in.at[way, t, q], code_send.at[t, q], code_recv.at[way, t, q],
            device_id={"space": jnp.where(way == 0, me + 1, me - 1)}, device_id_type=MESH)

    def head_copy(way, t, q):
        return pltpu.make_async_remote_copy(
            head.at[t, q], head_in.at[way, t, q], head_send.at[t, q], head_recv.at[way, t, q],
            device_id={"space": jnp.where(way == 0, me + 1, me - 1)}, device_id_type=MESH)

    def received(way, t, q):
        head_copy(way, t, q).wait_recv()
        chunk_copy(way, t, q).wait_recv()
        value = code_in[way, t, q].astype(jnp.int32).astype(jnp.float32) * head_in[way, t, q]
        return value.reshape(piece, spins, vectors)

    def emit(way, i):
        far, t, k = i // blocks, (i // pieces) % slices, i % pieces
        d = jnp.where(way == 0, n - 1 - far, far)
        q = d * pieces + k
        partial_sum(t, q, part)

        @pl.when(jnp.where(way == 0, me, mirror) > 0)
        def _():
            part[...] += received(way, t, q)

        x = part[...].reshape(rows, vectors)
        top = jnp.maximum(jnp.max(jnp.abs(x), axis=0, keepdims=True), 1e-30)
        head[t, q] = top * (1.0 / LEVELS)
        code[t, q] = jnp.round(x * (LEVELS / top)).astype(jnp.int32).astype(jnp.int16)
        head_copy(way, t, q).start()
        chunk_copy(way, t, q).start()

    lower = me < n // 2
    early = jnp.where(lower, 0, 1)
    late = 1 - early
    lead = blocks * jnp.where(lower, mirror - me, me - mirror)
    many = blocks * jnp.where(lower, mirror, me)
    few = blocks * jnp.where(lower, me, mirror)

    def emit_step(j):
        if slices > 1:
            @pl.when(j == pieces)
            def _():
                for t in range(1, slices):
                    wait_eigs(t)

        @pl.when((j >= lead) & (j - lead < few))
        def _():
            emit(late, j - lead)

        @pl.when(j < many)
        def _():
            emit(early, j)

    each(blocks * (n - 1), emit_step)

    each(blocks, lambda j: partial_sum(j // pieces, me * pieces + j % pieces, own.at[j // pieces, j % pieces]))

    @pl.when(jnp.where(lower, mirror, me) > 0)
    def _():
        def body(j):
            t, i = j // pieces, j % pieces
            own[t, i] += received(late, t, me * pieces + i)
        each(blocks, body)

    def finish(j):
        t, i = j // pieces, j % pieces

        @pl.when(jnp.where(lower, me, mirror) > 0)
        def _():
            own[t, i] += received(early, t, me * pieces + i)

        now = lax.axis_index("tm") * slices + t
        for b in range(piece):
            sign = jnp.where(now < time_ref[me * owned + i * piece + b], -1.0, 1.0)
            out_ref[t, i * piece + b] = (own[t, i, b] * sign).astype(jnp.bfloat16)

    each(blocks, finish)

    def drain_eigs(i):
        for c in range(2):
            for way in range(2):
                t, d, s, valid = message(way, i)

                @pl.when(valid)
                def _():
                    eig_copy(way, t, d, c, s).wait_send()

    each(messages, drain_eigs)

    def drain(j):
        t, q = j // (n * pieces), j % (n * pieces)
        d = q // pieces

        @pl.when(d != me)
        def _():
            way = jnp.where(d > me, 0, 1)
            head_copy(way, t, q).wait_send()
            chunk_copy(way, t, q).wait_send()

    each(slices * n * pieces, drain)


def shards(n, solutions, eigvecs, source_time):
    slices, sources, spins, cols = solutions.shape
    count = eigvecs.shape[2]
    vectors = n * count
    owned = sources // n
    pieces = PIECES if owned % PIECES == 0 else 1
    piece = owned // pieces
    blocks = n * pieces
    dma = pltpu.SemaphoreType.DMA
    result = jax.ShapeDtypeStruct((slices, owned, spins, vectors), jnp.bfloat16)
    return pl.pallas_call(
        functools.partial(kernel, n, pieces),
        out_shape=result,
        in_specs=[
            pl.BlockSpec(memory_space=pltpu.HBM),
            pl.BlockSpec(memory_space=pltpu.HBM),
            pl.BlockSpec(memory_space=pltpu.HBM),
        ],
        out_specs=pl.BlockSpec(memory_space=pltpu.VMEM),
        scratch_shapes=[
            pltpu.SMEM(source_time.shape, jnp.int32),
            pltpu.VMEM((slices, n, 2, n, count, cols), jnp.bfloat16),
            pltpu.VMEM((slices, sources, spins, cols), jnp.bfloat16),
            pltpu.VMEM((piece, spins, vectors), jnp.float32),
            pltpu.VMEM((slices, pieces, piece, spins, vectors), jnp.float32),
            pltpu.VMEM((slices, blocks, piece * spins, vectors), jnp.int16),
            pltpu.VMEM((2, slices, blocks, piece * spins, vectors), jnp.int16),
            pltpu.VMEM((slices, blocks, 1, vectors), jnp.float32),
            pltpu.VMEM((2, slices, blocks, 1, vectors), jnp.float32),
            dma,
            dma((slices, n)),
            dma((slices, n)),
            dma((slices, n, 2, n)),
            dma((slices, n, 2, n)),
            dma((slices, blocks)),
            dma((2, slices, blocks)),
            dma((slices, blocks)),
            dma((2, slices, blocks)),
        ],
        compiler_params=pltpu.CompilerParams(
            collective_id=0, has_side_effects=True, vmem_limit_bytes=VMEM_BYTES - result.size * 2),
    )(source_time, solutions, eigvecs)


def solution(mesh):
    return jax.shard_map(
        functools.partial(shards, mesh.shape["space"]),
        mesh=mesh,
        in_specs=(
            P(("cfg", "tm"), None, None, "space"),
            P(("cfg", "tm"), None, "space", None),
            P("cfg"),
        ),
        out_specs=P(("cfg", "tm"), "space", None, None),
        check_vma=False,
    )
```

time: 55.2 us -> 55.1 us (level)
  the two profiles are of different devices: /device:TPU:0 before, /device:TPU:16 now
where the time goes in v1:
time: 55.1 us; the launch traced here: 54.9 us
  Pallas kernels  53.1 us (96%)
  local copies, waits for them, and re-layouts  1.87 us (3%)
    pallas_call x1, Pallas kernels, shards(): pl.pallas_call(functools.partial(kernel, n, pieces), out_shape=result, in...  53.1 us
    unnamed x1, local copies, waits for them, and re-layouts  1.87 us

profile of v1, /device:TPU:16, one launch (start us, length us, event | category | flops | bytes accessed | tf_op | source)
XLA Modules:
  0.0 54.9 jit_solution(17976657101988991208)
XLA Ops:
  0.0 53.1 %shard_map.37 = bf16[2,32,32,128]{3,2,1,0:T(8,128)(2,1)} custom-call(s32[128]{0:T(128)} %time_hbm.1, bf16[2,128,32,768]{3,2,1,0:T(8,128)(2,1)} %sol_hbm.1, bf16[2,2,32,3072]{3,2,1,0:T(8,128)(2,1)} %eig_hbm.1), custom_call_target="tpu_custom_call" | custom-call | tf_op jit(solution)/shard_map/pallas_call | solution.py:232
  53.1 1.9 %copy.5 = bf16[2,32,32,128]{3,2,1,0:T(8,128)(2,1)} copy(bf16[2,32,32,128]{3,2,1,0:T(8,128)(2,1)} %shard_map.37) | data formatting | bytes 1048576

commit v2 on v1

--- a/solution.py
+++ b/solution.py
@@ -10,11 +10,11 @@
 MESH = pl.DeviceIdType.MESH
 LEVELS = 32767.0
 PIECES = 1
-VMEM_BYTES = 67043328
-
-
-def kernel(n, pieces, time_hbm, sol_hbm, eig_hbm, out_ref, time_ref, eig_v, sol_v, part, own, code, code_in, head,
-           head_in, time_sem, load_sem, sol_sem, eig_send, eig_recv, code_send, code_recv, head_send, head_recv):
+VMEM_BYTES = 48 << 20
+
+
+def kernel(n, pieces, time_hbm, sol_hbm, eig_hbm, out_ref, time_ref, eig_v, sol_v, sign, part, own, code, code_in,
+           head, head_in, time_sem, load_sem, sol_sem, eig_send, eig_recv, code_send, code_recv, head_send, head_recv):
     me = lax.axis_index("space")
     slices, sources, spins, cols = sol_v.shape
     count = eig_v.shape[4]
@@ -58,10 +58,16 @@
             return 0
         lax.fori_loop(0, total, step, 0)
 
-    each(slices * n, lambda i: eig_load(i % slices, i // slices).start())
+    def load_eigs(i):
+        far, t = i // slices, i % slices
+        for d in (n - 1 - far, far):
+            eig_load(t, d).start()
+
+    each(slices * (n // 2), load_eigs)
+    if n % 2:
+        each(slices, lambda t: eig_load(t, n // 2).start())
     time_copy = pltpu.make_async_copy(time_hbm, time_ref, time_sem)
     time_copy.start()
-    each(slices * n, lambda i: eig_load(i % slices, i // slices).wait())
     pl.semaphore_wait(barrier, jnp.where((me > 0) & (mirror > 0), 2, 1))
 
     def message(way, i):
@@ -83,6 +89,11 @@
                     def _():
                         eig_copy(way, t, d, c, s).wait_recv()
 
+                    if c == 0:
+                        @pl.when(s == me)
+                        def _():
+                            eig_load(t, d).wait()
+
                     eig_copy(way, t, d, c, s).start()
 
     send_eigs(0)
@@ -91,6 +102,8 @@
     each(messages - 1, lambda i: send_eigs(i + 1))
 
     def wait_eigs(t):
+        eig_load(t, me).wait()
+
         def body(i):
             s = i // 2
 
@@ -102,7 +115,6 @@
 
     wait_eigs(0)
     each(slices * n, lambda i: sol_copy(i // n, i % n).wait())
-    time_copy.wait()
 
     def partial_sum(t, q, dst):
         block = sol_v[t, pl.ds(q * piece, piece)].reshape(rows, cols)
@@ -172,6 +184,15 @@
 
     each(blocks * (n - 1), emit_step)
 
+    time_copy.wait()
+
+    def set_sign(j):
+        t, b = j // owned, j % owned
+        now = lax.axis_index("tm") * slices + t
+        value = jnp.where(now < time_ref[me * owned + b], -1.0, 1.0)
+        sign[t, b] = jnp.full((1, vectors), value, jnp.float32)
+
+    each(slices * owned, set_sign)
     each(blocks, lambda j: partial_sum(j // pieces, me * pieces + j % pieces, own.at[j // pieces, j % pieces]))
 
     @pl.when(jnp.where(lower, mirror, me) > 0)
@@ -181,20 +202,6 @@
             own[t, i] += received(late, t, me * pieces + i)
         each(blocks, body)
 
-    def finish(j):
-        t, i = j // pieces, j % pieces
-
-        @pl.when(jnp.where(lower, me, mirror) > 0)
-        def _():
-            own[t, i] += received(early, t, me * pieces + i)
-
-        now = lax.axis_index("tm") * slices + t
-        for b in range(piece):
-            sign = jnp.where(now < time_ref[me * owned + i * piece + b], -1.0, 1.0)
-            out_ref[t, i * piece + b] = (own[t, i, b] * sign).astype(jnp.bfloat16)
-
-    each(blocks, finish)
-
     def drain_eigs(i):
         for c in range(2):
             for way in range(2):
@@ -217,6 +224,18 @@
             chunk_copy(way, t, q).wait_send()
 
     each(slices * n * pieces, drain)
+
+    def finish(j):
+        t, i = j // pieces, j % pieces
+
+        @pl.when(jnp.where(lower, me, mirror) > 0)
+        def _():
+            own[t, i] += received(early, t, me * pieces + i)
+
+        mine = pl.ds(i * piece, piece)
+        out_ref[t, mine] = (own[t, i] * sign[t, mine]).astype(jnp.bfloat16)
+
+    each(blocks, finish)
 
 
 def shards(n, solutions, eigvecs, source_time):
@@ -242,6 +261,7 @@
             pltpu.SMEM(source_time.shape, jnp.int32),
             pltpu.VMEM((slices, n, 2, n, count, cols), jnp.bfloat16),
             pltpu.VMEM((slices, sources, spins, cols), jnp.bfloat16),
+            pltpu.VMEM((slices, owned, 1, vectors), jnp.float32),
             pltpu.VMEM((piece, spins, vectors), jnp.float32),
             pltpu.VMEM((slices, pieces, piece, spins, vectors), jnp.float32),
             pltpu.VMEM((slices, blocks, piece * spins, vectors), jnp.int16),
@@ -259,8 +279,8 @@
             dma((2, slices, blocks)),
         ],
         compiler_params=pltpu.CompilerParams(
-            collective_id=0, has_side_effects=True, vmem_limit_bytes=VMEM_BYTES - result.size * 2),
-    )(source_time, solutions, eigvecs)
+            collective_id=0, has_side_effects=True, vmem_limit_bytes=VMEM_BYTES),
+    )(*(pltpu.with_memory_space_constraint(x, pltpu.HBM) for x in (source_time, solutions, eigvecs)))
 
 
 def solution(mesh):

time: 55.1 us -> 52.4 us (0.951)
  the two profiles are of different devices: /device:TPU:16 before, /device:TPU:0 now
where the time goes in v2:
time: 52.4 us; the launch traced here: 52 us
  Pallas kernels  51.2 us (98%)
  local copies, waits for them, and re-layouts  0.8 us (2%)
    pallas_call x1, Pallas kernels, shards(): pl.pallas_call(functools.partial(kernel, n, pieces), out_shape=result, in...  51.2 us

profile of v2, /device:TPU:0, one launch (start us, length us, event | category | flops | bytes accessed | tf_op | source)
XLA Modules:
  0.0 52.0 jit_solution(12158643779850177030)
XLA Ops:
  0.0 51.2 %shard_map.37 = bf16[2,32,32,128]{3,2,1,0:T(8,128)(2,1)S(1)} custom-call(s32[128]{0:T(128)} %time_hbm.1, bf16[2,128,32,768]{3,2,1,0:T(8,128)(2,1)} %sol_hbm.1, bf16[2,2,32,3072]{3,2,1,0:T(8,128)(2,1)} %eig_hbm.1), custom_call_target="tpu_custom_call" | custom-call | tf_op jit(solution)/shard_map/pallas_call | solution.py:251
  51.2 0.8 %copy.5 = bf16[2,32,32,128]{3,2,1,0:T(8,128)(2,1)} copy(bf16[2,32,32,128]{3,2,1,0:T(8,128)(2,1)S(1)} %shard_map.37) | data formatting | bytes 1048576

commit v3 on v2

--- a/solution.py
+++ b/solution.py
@@ -52,6 +52,12 @@
             eig_v.at[t, d, c, s], eig_v.at[t, d, c, s], eig_send.at[t, d, c, s], eig_recv.at[t, d, c, s],
             device_id={"space": next_of(way)}, device_id_type=MESH)
 
+    def first_copy(way, t, d, c, s):
+        block = pl.ds(pl.multiple_of(d * cols, cols), cols)
+        return pltpu.make_async_remote_copy(
+            eig_hbm.at[t, c, :, block], eig_v.at[t, d, c, s], eig_send.at[t, d, c, s], eig_recv.at[t, d, c, s],
+            device_id={"space": next_of(way)}, device_id_type=MESH)
+
     def each(total, body):
         def step(i, _):
             body(i)
@@ -61,7 +67,9 @@
     def load_eigs(i):
         far, t = i // slices, i % slices
         for d in (n - 1 - far, far):
-            eig_load(t, d).start()
+            @pl.when((t > 0) | (d == me) | ((d != 0) & (d != n - 1)))
+            def _():
+                eig_load(t, d).start()
 
     each(slices * (n // 2), load_eigs)
     if n % 2:
@@ -96,7 +104,14 @@
 
                     eig_copy(way, t, d, c, s).start()
 
-    send_eigs(0)
+    for c in range(2):
+        for way in range(2):
+            t, d, s, valid = message(way, 0)
+
+            @pl.when(valid)
+            def _():
+                first_copy(way, t, d, c, s).start()
+
     each(slices * n, lambda i: sol_copy(i // n, i % n).start())
     messages = slices * ((n * n) // 4)
     each(messages - 1, lambda i: send_eigs(i + 1))
@@ -202,6 +217,16 @@
             own[t, i] += received(late, t, me * pieces + i)
         each(blocks, body)
 
+    def finish(j):
+        t, i = j // pieces, j % pieces
+
+        @pl.when(jnp.where(lower, me, mirror) > 0)
+        def _():
+            own[t, i] += received(early, t, me * pieces + i)
+
+        mine = pl.ds(i * piece, piece)
+        out_ref[t, mine] = (own[t, i] * sign[t, mine]).astype(jnp.bfloat16)
+
     def drain_eigs(i):
         for c in range(2):
             for way in range(2):
@@ -211,7 +236,6 @@
                 def _():
                     eig_copy(way, t, d, c, s).wait_send()
 
-    each(messages, drain_eigs)
 
     def drain(j):
         t, q = j // (n * pieces), j % (n * pieces)
@@ -223,19 +247,18 @@
             head_copy(way, t, q).wait_send()
             chunk_copy(way, t, q).wait_send()
 
+    outer = (me == 0) | (mirror == 0)
+
+    @pl.when(outer)
+    def _():
+        each(blocks, finish)
+
+    each(messages, drain_eigs)
     each(slices * n * pieces, drain)
 
-    def finish(j):
-        t, i = j // pieces, j % pieces
-
-        @pl.when(jnp.where(lower, me, mirror) > 0)
-        def _():
-            own[t, i] += received(early, t, me * pieces + i)
-
-        mine = pl.ds(i * piece, piece)
-        out_ref[t, mine] = (own[t, i] * sign[t, mine]).astype(jnp.bfloat16)
-
-    each(blocks, finish)
+    @pl.when(jnp.logical_not(outer))
+    def _():
+        each(blocks, finish)
 
 
 def shards(n, solutions, eigvecs, source_time):

time: 52.4 us -> 52.3 us (level)
  no operation moved by 1% of the time
where the time goes in v3:
time: 52.3 us; the launch traced here: 52.2 us
  Pallas kernels  51.4 us (98%)
  local copies, waits for them, and re-layouts  0.8 us (2%)
    pallas_call x1, Pallas kernels, shards(): pl.pallas_call(functools.partial(kernel, n, pieces), out_shape=result, in...  51.4 us

profile of v3, /device:TPU:0, one launch (start us, length us, event | category | flops | bytes accessed | tf_op | source)
XLA Modules:
  0.0 52.2 jit_solution(7437746526326507046)
XLA Ops:
  0.0 51.4 %shard_map.37 = bf16[2,32,32,128]{3,2,1,0:T(8,128)(2,1)S(1)} custom-call(s32[128]{0:T(128)} %time_hbm.1, bf16[2,128,32,768]{3,2,1,0:T(8,128)(2,1)} %sol_hbm.1, bf16[2,2,32,3072]{3,2,1,0:T(8,128)(2,1)} %eig_hbm.1), custom_call_target="tpu_custom_call" | custom-call | tf_op jit(solution)/shard_map/pallas_call | solution.py:274
  51.4 0.8 %copy.5 = bf16[2,32,32,128]{3,2,1,0:T(8,128)(2,1)} copy(bf16[2,32,32,128]{3,2,1,0:T(8,128)(2,1)S(1)} %shard_map.37) | data formatting | bytes 1048576

commit v4 on v3

--- a/solution.py
+++ b/solution.py
@@ -34,7 +34,7 @@
     def behind(way):
         return me if way == 0 else mirror
 
-    for way in range(2):
+    for way in (1, 0):
         @pl.when(behind(1 - way) > 0)
         def _():
             pl.semaphore_signal(barrier, inc=1, device_id={"space": next_of(way)}, device_id_type=MESH)
@@ -63,6 +63,23 @@
             body(i)
             return 0
         lax.fori_loop(0, total, step, 0)
+
+    @pl.when(me == 0)
+    def _():
+        eig_load(0, n - 1).start()
+
+    pl.semaphore_wait(barrier, jnp.where((me > 0) & (mirror > 0), 2, 1))
+    @pl.when(me == 0)
+    def _():
+        eig_load(0, n - 1).wait()
+        for c in range(2):
+            eig_copy(0, 0, n - 1, c, me).start()
+
+    for c in range(2):
+        for way in range(2):
+            @pl.when((behind(1 - way) > 0) & (me > 0))
+            def _():
+                first_copy(way, 0, n - 1 if way == 0 else 0, c, me).start()
 
     def load_eigs(i):
         far, t = i // slices, i % slices
@@ -76,7 +93,6 @@
         each(slices, lambda t: eig_load(t, n // 2).start())
     time_copy = pltpu.make_async_copy(time_hbm, time_ref, time_sem)
     time_copy.start()
-    pl.semaphore_wait(barrier, jnp.where((me > 0) & (mirror > 0), 2, 1))
 
     def message(way, i):
         members = behind(way) + 1
@@ -103,14 +119,6 @@
                             eig_load(t, d).wait()
 
                     eig_copy(way, t, d, c, s).start()
-
-    for c in range(2):
-        for way in range(2):
-            t, d, s, valid = message(way, 0)
-
-            @pl.when(valid)
-            def _():
-                first_copy(way, t, d, c, s).start()
 
     each(slices * n, lambda i: sol_copy(i // n, i % n).start())
     messages = slices * ((n * n) // 4)
@@ -219,13 +227,17 @@
 
     def finish(j):
         t, i = j // pieces, j % pieces
-
-        @pl.when(jnp.where(lower, me, mirror) > 0)
-        def _():
-            own[t, i] += received(early, t, me * pieces + i)
-
         mine = pl.ds(i * piece, piece)
-        out_ref[t, mine] = (own[t, i] * sign[t, mine]).astype(jnp.bfloat16)
+        inner = jnp.where(lower, me, mirror) > 0
+
+        @pl.when(inner)
+        def _():
+            total = own[t, i] + received(early, t, me * pieces + i)
+            out_ref[t, mine] = (total * sign[t, mine]).astype(jnp.bfloat16)
+
+        @pl.when(jnp.logical_not(inner))
+        def _():
+            out_ref[t, mine] = (own[t, i] * sign[t, mine]).astype(jnp.bfloat16)
 
     def drain_eigs(i):
         for c in range(2):

time: 52.3 us -> 52.1 us (level)
  no operation moved by 1% of the time
where the time goes in v4:
time: 52.1 us; the launch traced here: 51.9 us
  Pallas kernels  51.1 us (98%)
  local copies, waits for them, and re-layouts  0.8 us (2%)
    pallas_call x1, Pallas kernels, shards(): pl.pallas_call(functools.partial(kernel, n, pieces), out_shape=result, in...  51.1 us

profile of v4, /device:TPU:0, one launch (start us, length us, event | category | flops | bytes accessed | tf_op | source)
XLA Modules:
  0.0 51.9 jit_solution(48985264707130640)
XLA Ops:
  0.0 51.1 %shard_map.37 = bf16[2,32,32,128]{3,2,1,0:T(8,128)(2,1)S(1)} custom-call(s32[128]{0:T(128)} %time_hbm.1, bf16[2,128,32,768]{3,2,1,0:T(8,128)(2,1)} %sol_hbm.1, bf16[2,2,32,3072]{3,2,1,0:T(8,128)(2,1)} %eig_hbm.1), custom_call_target="tpu_custom_call" | custom-call | tf_op jit(solution)/shard_map/pallas_call | solution.py:286
  51.2 0.8 %copy.5 = bf16[2,32,32,128]{3,2,1,0:T(8,128)(2,1)} copy(bf16[2,32,32,128]{3,2,1,0:T(8,128)(2,1)S(1)} %shard_map.37) | data formatting | bytes 1048576

commit v5 on v4

--- a/solution.py
+++ b/solution.py
@@ -10,11 +10,14 @@
 MESH = pl.DeviceIdType.MESH
 LEVELS = 32767.0
 PIECES = 1
+SHARE = 2
+HELD = 2
 VMEM_BYTES = 48 << 20
 
 
-def kernel(n, pieces, time_hbm, sol_hbm, eig_hbm, out_ref, time_ref, eig_v, sol_v, sign, part, own, code, code_in,
-           head, head_in, time_sem, load_sem, sol_sem, eig_send, eig_recv, code_send, code_recv, head_send, head_recv):
+def kernel(n, pieces, paired, time_hbm, sol_hbm, eig_hbm, out_ref, time_ref, eig_v, sol_v, sign, part, own, code, code_in,
+           head, head_in, relay, time_sem, load_sem, sol_sem, eig_send, eig_recv, code_send, code_recv, head_send, head_recv,
+           relay_send, relay_recv, relay_hop, relay_land, relay_ready):
     me = lax.axis_index("space")
     slices, sources, spins, cols = sol_v.shape
     count = eig_v.shape[4]
@@ -25,6 +28,12 @@
     half = spins // 2
     blocks = slices * pieces
     mirror = n - 1 - me
+    outer = (me == 0) | (mirror == 0)
+    tm = lax.axis_index("tm")
+    hands = (me == 0) & (tm % 2 == 0)
+    helps = (me == 0) & (tm % 2 == 1)
+    inward = 1
+    kept = rows - relay.shape[0]
 
     barrier = pltpu.get_barrier_semaphore()
 
@@ -38,6 +47,11 @@
         @pl.when(behind(1 - way) > 0)
         def _():
             pl.semaphore_signal(barrier, inc=1, device_id={"space": next_of(way)}, device_id_type=MESH)
+
+    if paired:
+        @pl.when(hands)
+        def _():
+            pl.semaphore_signal(barrier, inc=1, device_id={"tm": tm + 1}, device_id_type=MESH)
 
     def eig_load(t, d):
         block = pl.ds(pl.multiple_of(d * cols, cols), cols)
@@ -68,7 +82,15 @@
     def _():
         eig_load(0, n - 1).start()
 
-    pl.semaphore_wait(barrier, jnp.where((me > 0) & (mirror > 0), 2, 1))
+    if paired:
+        pl.semaphore_wait(barrier, jnp.where(outer & jnp.logical_not(helps), 1, 2))
+
+        @pl.when(helps)
+        def _():
+            pl.semaphore_signal(relay_ready, inc=1, device_id={"tm": tm - 1}, device_id_type=MESH)
+    else:
+        pl.semaphore_wait(barrier, jnp.where(outer, 1, 2))
+
     @pl.when(me == 0)
     def _():
         eig_load(0, n - 1).wait()
@@ -160,16 +182,48 @@
             head.at[t, q], head_in.at[way, t, q], head_send.at[t, q], head_recv.at[way, t, q],
             device_id={"space": jnp.where(way == 0, me + 1, me - 1)}, device_id_type=MESH)
 
+    def kept_copy(way, t, q):
+        part = pl.ds(0, kept)
+        return pltpu.make_async_remote_copy(
+            code.at[t, q, part], code_in.at[way, t, q, part], code_send.at[t, q], code_recv.at[way, t, q],
+            device_id={"space": jnp.where(way == 0, me + 1, me - 1)}, device_id_type=MESH)
+
+    def relay_push(t, q):
+        return pltpu.make_async_remote_copy(
+            code.at[t, q, pl.ds(kept, rows - kept)], relay, relay_send, relay_recv,
+            device_id={"tm": tm + 1}, device_id_type=MESH)
+
+    def relay_on(way, t, q):
+        return pltpu.make_async_remote_copy(
+            relay, code_in.at[way, t, q, pl.ds(kept, rows - kept)], relay_hop, relay_land.at[way],
+            device_id={"space": inward, "tm": tm - 1}, device_id_type=MESH)
+
     def received(way, t, q):
         head_copy(way, t, q).wait_recv()
-        chunk_copy(way, t, q).wait_recv()
+        if paired:
+            parted = (tm % 2 == 0) & (me == 1) & (way == 0) & (t == slices - 1) & (q == me * pieces + pieces - 1)
+
+            @pl.when(parted)
+            def _():
+                kept_copy(way, t, q).wait_recv()
+                relay_on(way, t, q).wait_recv()
+
+            @pl.when(jnp.logical_not(parted))
+            def _():
+                chunk_copy(way, t, q).wait_recv()
+        else:
+            chunk_copy(way, t, q).wait_recv()
         value = code_in[way, t, q].astype(jnp.int32).astype(jnp.float32) * head_in[way, t, q]
         return value.reshape(piece, spins, vectors)
 
+    final = blocks * (n - 1) - 1
+
+    def place(way, i):
+        far, t, k = i // blocks, (i // pieces) % slices, i % pieces
+        return t, jnp.where(way == 0, n - 1 - far, far) * pieces + k
+
     def emit(way, i):
-        far, t, k = i // blocks, (i // pieces) % slices, i % pieces
-        d = jnp.where(way == 0, n - 1 - far, far)
-        q = d * pieces + k
+        t, q = place(way, i)
         partial_sum(t, q, part)
 
         @pl.when(jnp.where(way == 0, me, mirror) > 0)
@@ -180,8 +234,19 @@
         top = jnp.maximum(jnp.max(jnp.abs(x), axis=0, keepdims=True), 1e-30)
         head[t, q] = top * (1.0 / LEVELS)
         code[t, q] = jnp.round(x * (LEVELS / top)).astype(jnp.int32).astype(jnp.int16)
-        head_copy(way, t, q).start()
-        chunk_copy(way, t, q).start()
+        if paired:
+            @pl.when((i == final) & helps)
+            def _():
+                relay_push(t, q).wait_recv()
+                relay_on(way, t, q).start()
+
+            @pl.when(jnp.logical_not(hands & (i >= final - HELD)))
+            def _():
+                head_copy(way, t, q).start()
+                chunk_copy(way, t, q).start()
+        else:
+            head_copy(way, t, q).start()
+            chunk_copy(way, t, q).start()
 
     lower = me < n // 2
     early = jnp.where(lower, 0, 1)
@@ -206,6 +271,21 @@
             emit(early, j)
 
     each(blocks * (n - 1), emit_step)
+    if paired:
+        @pl.when(hands)
+        def _():
+            pl.semaphore_wait(relay_ready, 1)
+            relay_push(*place(early, final)).start()
+
+            def start_held(j):
+                at = place(early, final - HELD + j)
+                head_copy(early, *at).start()
+                chunk_copy(early, *at).start()
+
+            each(HELD, start_held)
+            at = place(early, final)
+            head_copy(early, *at).start()
+            kept_copy(early, *at).start()
 
     time_copy.wait()
 
@@ -257,9 +337,23 @@
         def _():
             way = jnp.where(d > me, 0, 1)
             head_copy(way, t, q).wait_send()
-            chunk_copy(way, t, q).wait_send()
-
-    outer = (me == 0) | (mirror == 0)
+            if paired:
+                last = (me == 0) & (t == slices - 1) & (q == inward * pieces + pieces - 1)
+
+                @pl.when(last & helps)
+                def _():
+                    relay_on(way, t, q).wait_send()
+
+                @pl.when(last & hands)
+                def _():
+                    relay_push(t, q).wait_send()
+                    kept_copy(way, t, q).wait_send()
+
+                @pl.when(jnp.logical_not(last & hands))
+                def _():
+                    chunk_copy(way, t, q).wait_send()
+            else:
+                chunk_copy(way, t, q).wait_send()
 
     @pl.when(outer)
     def _():
@@ -273,7 +367,7 @@
         each(blocks, finish)
 
 
-def shards(n, solutions, eigvecs, source_time):
+def shards(n, cores, solutions, eigvecs, source_time):
     slices, sources, spins, cols = solutions.shape
     count = eigvecs.shape[2]
     vectors = n * count
@@ -284,7 +378,7 @@
     dma = pltpu.SemaphoreType.DMA
     result = jax.ShapeDtypeStruct((slices, owned, spins, vectors), jnp.bfloat16)
     return pl.pallas_call(
-        functools.partial(kernel, n, pieces),
+        functools.partial(kernel, n, pieces, cores % 2 == 0),
         out_shape=result,
         in_specs=[
             pl.BlockSpec(memory_space=pltpu.HBM),
@@ -303,6 +397,7 @@
             pltpu.VMEM((2, slices, blocks, piece * spins, vectors), jnp.int16),
             pltpu.VMEM((slices, blocks, 1, vectors), jnp.float32),
             pltpu.VMEM((2, slices, blocks, 1, vectors), jnp.float32),
+            pltpu.VMEM((piece * spins // SHARE, vectors), jnp.int16),
             dma,
             dma((slices, n)),
             dma((slices, n)),
@@ -312,6 +407,11 @@
             dma((2, slices, blocks)),
             dma((slices, blocks)),
             dma((2, slices, blocks)),
+            dma,
+            dma,
+            dma,
+            dma((2,)),
+            pltpu.SemaphoreType.REGULAR,
         ],
         compiler_params=pltpu.CompilerParams(
             collective_id=0, has_side_effects=True, vmem_limit_bytes=VMEM_BYTES),
@@ -320,7 +420,7 @@
 
 def solution(mesh):
     return jax.shard_map(
-        functools.partial(shards, mesh.shape["space"]),
+        functools.partial(shards, mesh.shape["space"], mesh.shape["tm"]),
         mesh=mesh,
         in_specs=(
             P(("cfg", "tm"), None, None, "space"),

time: 52.1 us -> 51.9 us (level); the launches traced: 51.9 us -> 51.1 us
  Pallas kernels: 51.1 us -> 50.3 us
    pallas_call x1, Pallas kernels: 51.1 us -> 50.3 us  [shards(): pl.pallas_call(functools.partial(kernel, n, pieces, cores % 2 == 0), out_...]
where the time goes in v5:
time: 51.9 us; the launch traced here: 51.1 us
  Pallas kernels  50.3 us (97%)
  local copies, waits for them, and re-layouts  0.8 us (2%)
    pallas_call x1, Pallas kernels, shards(): pl.pallas_call(functools.partial(kernel, n, pieces, cores % 2 == 0), out_...  50.3 us

profile of v5, /device:TPU:0, one launch (start us, length us, event | category | flops | bytes accessed | tf_op | source)
XLA Modules:
  0.0 51.1 jit_solution(14922802990817475728)
XLA Ops:
  0.0 50.3 %shard_map.37 = bf16[2,32,32,128]{3,2,1,0:T(8,128)(2,1)S(1)} custom-call(s32[128]{0:T(128)} %time_hbm.1, bf16[2,128,32,768]{3,2,1,0:T(8,128)(2,1)} %sol_hbm.1, bf16[2,2,32,3072]{3,2,1,0:T(8,128)(2,1)} %eig_hbm.1), custom_call_target="tpu_custom_call" | custom-call | tf_op jit(solution)/shard_map/pallas_call | solution.py:380
  50.3 0.8 %copy.5 = bf16[2,32,32,128]{3,2,1,0:T(8,128)(2,1)} copy(bf16[2,32,32,128]{3,2,1,0:T(8,128)(2,1)S(1)} %shard_map.37) | data formatting | bytes 1048576

commit v6 on v5

--- a/solution.py
+++ b/solution.py
@@ -17,7 +17,7 @@
 
 def kernel(n, pieces, paired, time_hbm, sol_hbm, eig_hbm, out_ref, time_ref, eig_v, sol_v, sign, part, own, code, code_in,
            head, head_in, relay, time_sem, load_sem, sol_sem, eig_send, eig_recv, code_send, code_recv, head_send, head_recv,
-           relay_send, relay_recv, relay_hop, relay_land, relay_ready):
+           relay_send, relay_recv, relay_hop, relay_land):
     me = lax.axis_index("space")
     slices, sources, spins, cols = sol_v.shape
     count = eig_v.shape[4]
@@ -30,9 +30,9 @@
     mirror = n - 1 - me
     outer = (me == 0) | (mirror == 0)
     tm = lax.axis_index("tm")
-    hands = (me == 0) & (tm % 2 == 0)
-    helps = (me == 0) & (tm % 2 == 1)
-    inward = 1
+    hands = outer & (tm % 2 == 0)
+    helps = outer & (tm % 2 == 1)
+    inward = jnp.where(me == 0, 1, n - 2)
     kept = rows - relay.shape[0]
 
     barrier = pltpu.get_barrier_semaphore()
@@ -49,9 +49,9 @@
             pl.semaphore_signal(barrier, inc=1, device_id={"space": next_of(way)}, device_id_type=MESH)
 
     if paired:
-        @pl.when(hands)
-        def _():
-            pl.semaphore_signal(barrier, inc=1, device_id={"tm": tm + 1}, device_id_type=MESH)
+        @pl.when(helps)
+        def _():
+            pl.semaphore_signal(barrier, inc=1, device_id={"tm": tm - 1}, device_id_type=MESH)
 
     def eig_load(t, d):
         block = pl.ds(pl.multiple_of(d * cols, cols), cols)
@@ -82,14 +82,7 @@
     def _():
         eig_load(0, n - 1).start()
 
-    if paired:
-        pl.semaphore_wait(barrier, jnp.where(outer & jnp.logical_not(helps), 1, 2))
-
-        @pl.when(helps)
-        def _():
-            pl.semaphore_signal(relay_ready, inc=1, device_id={"tm": tm - 1}, device_id_type=MESH)
-    else:
-        pl.semaphore_wait(barrier, jnp.where(outer, 1, 2))
+    pl.semaphore_wait(barrier, jnp.where(outer & jnp.logical_not(hands & paired), 1, 2))
 
     @pl.when(me == 0)
     def _():
@@ -201,7 +194,8 @@
     def received(way, t, q):
         head_copy(way, t, q).wait_recv()
         if paired:
-            parted = (tm % 2 == 0) & (me == 1) & (way == 0) & (t == slices - 1) & (q == me * pieces + pieces - 1)
+            from_end = jnp.where(way == 0, me == 1, mirror == 1)
+            parted = (tm % 2 == 0) & from_end & (t == slices - 1) & (q == me * pieces + pieces - 1)
 
             @pl.when(parted)
             def _():
@@ -274,7 +268,6 @@
     if paired:
         @pl.when(hands)
         def _():
-            pl.semaphore_wait(relay_ready, 1)
             relay_push(*place(early, final)).start()
 
             def start_held(j):
@@ -338,7 +331,7 @@
             way = jnp.where(d > me, 0, 1)
             head_copy(way, t, q).wait_send()
             if paired:
-                last = (me == 0) & (t == slices - 1) & (q == inward * pieces + pieces - 1)
+                last = outer & (t == slices - 1) & (q == inward * pieces + pieces - 1)
 
                 @pl.when(last & helps)
                 def _():
@@ -411,7 +404,6 @@
             dma,
             dma,
             dma((2,)),
-            pltpu.SemaphoreType.REGULAR,
         ],
         compiler_params=pltpu.CompilerParams(
             collective_id=0, has_side_effects=True, vmem_limit_bytes=VMEM_BYTES),

time: 51.9 us -> 51.9 us (level)
  no operation moved by 1% of the time
where the time goes in v6:
time: 51.9 us; the launch traced here: 51.1 us
  Pallas kernels  50.3 us (97%)
  local copies, waits for them, and re-layouts  0.8 us (2%)
    pallas_call x1, Pallas kernels, shards(): pl.pallas_call(functools.partial(kernel, n, pieces, cores % 2 == 0), out_...  50.3 us

profile of v6, /device:TPU:0, one launch (start us, length us, event | category | flops | bytes accessed | tf_op | source)
XLA Modules:
  0.0 51.1 jit_solution(10940247615883183284)
XLA Ops:
  0.0 50.3 %shard_map.37 = bf16[2,32,32,128]{3,2,1,0:T(8,128)(2,1)S(1)} custom-call(s32[128]{0:T(128)} %time_hbm.1, bf16[2,128,32,768]{3,2,1,0:T(8,128)(2,1)} %sol_hbm.1, bf16[2,2,32,3072]{3,2,1,0:T(8,128)(2,1)} %eig_hbm.1), custom_call_target="tpu_custom_call" | custom-call | tf_op jit(solution)/shard_map/pallas_call | solution.py:373
  50.3 0.8 %copy.5 = bf16[2,32,32,128]{3,2,1,0:T(8,128)(2,1)} copy(bf16[2,32,32,128]{3,2,1,0:T(8,128)(2,1)S(1)} %shard_map.37) | data formatting | bytes 1048576

commit v7 on v6

--- a/solution.py
+++ b/solution.py
@@ -11,7 +11,7 @@
 LEVELS = 32767.0
 PIECES = 1
 SHARE = 2
-HELD = 2
+HELD = 1
 VMEM_BYTES = 48 << 20
 
 
@@ -211,6 +211,7 @@
         return value.reshape(piece, spins, vectors)
 
     final = blocks * (n - 1) - 1
+    held = min(HELD, final)
 
     def place(way, i):
         far, t, k = i // blocks, (i // pieces) % slices, i % pieces
@@ -234,7 +235,7 @@
                 relay_push(t, q).wait_recv()
                 relay_on(way, t, q).start()
 
-            @pl.when(jnp.logical_not(hands & (i >= final - HELD)))
+            @pl.when(jnp.logical_not(hands & (i >= final - held)))
             def _():
                 head_copy(way, t, q).start()
                 chunk_copy(way, t, q).start()
@@ -271,11 +272,11 @@
             relay_push(*place(early, final)).start()
 
             def start_held(j):
-                at = place(early, final - HELD + j)
+                at = place(early, final - held + j)
                 head_copy(early, *at).start()
                 chunk_copy(early, *at).start()
 
-            each(HELD, start_held)
+            each(held, start_held)
             at = place(early, final)
             head_copy(early, *at).start()
             kept_copy(early, *at).start()

time: 51.9 us -> 51.9 us (level)
  no operation moved by 1% of the time
where the time goes in v7:
time: 51.9 us; the launch traced here: 51.1 us
  Pallas kernels  50.3 us (97%)
  local copies, waits for them, and re-layouts  0.8 us (2%)
    pallas_call x1, Pallas kernels, shards(): pl.pallas_call(functools.partial(kernel, n, pieces, cores % 2 == 0), out_...  50.3 us

profile of v7, /device:TPU:0, one launch (start us, length us, event | category | flops | bytes accessed | tf_op | source)
XLA Modules:
  0.0 51.1 jit_solution(17660136895138674150)
XLA Ops:
  0.0 50.3 %shard_map.37 = bf16[2,32,32,128]{3,2,1,0:T(8,128)(2,1)S(1)} custom-call(s32[128]{0:T(128)} %time_hbm.1, bf16[2,128,32,768]{3,2,1,0:T(8,128)(2,1)} %sol_hbm.1, bf16[2,2,32,3072]{3,2,1,0:T(8,128)(2,1)} %eig_hbm.1), custom_call_target="tpu_custom_call" | custom-call | tf_op jit(solution)/shard_map/pallas_call | solution.py:374
  50.3 0.8 %copy.5 = bf16[2,32,32,128]{3,2,1,0:T(8,128)(2,1)} copy(bf16[2,32,32,128]{3,2,1,0:T(8,128)(2,1)S(1)} %shard_map.37) | data formatting | bytes 1048576
